TPU v7x, 256 devices: a whole 4x4x8 slice. The times are simulated.
256 devices in a mesh: segment: 16 (over z, x_lo), dp: 16 (over y, x_hi, core).
Axes of the slice: x: 4 (x_hi: 2, x_lo: 2; x = x_hi * 2 + x_lo), y: 4, z: 8, core: 2. Of those that a mesh axis runs over, the one named last changes fastest.
Arguments:
- src_embed: bfloat16 [64, 128, 2048], P('dp', None, 'segment'), parts along dimension 0, may hold values from -6 to 6
- tgt_embed: bfloat16 [64, 128, 2048], P('dp', None, 'segment'), parts along dimension 0, may hold values from -6 to 6
- src_lengths: int32 [64], P('dp'), parts along dimension 0, may hold values from 32 to 128
- tgt_lengths: int32 [64], P('dp'), parts along dimension 0, may hold values from 32 to 128
- attn_in: bfloat16 [16, 2048, 1536], P('segment'), may hold values from -0.125 to 0.125
- attn_out: bfloat16 [16, 512, 2048], P('segment'), may hold values from -0.375 to 0.375
- norm_gain: float32 [4, 2048], replicated, may hold values from 0.25 to 1.75
- final_gain: float32 [2048], replicated, may hold values from 0.25 to 1.75
Outputs:
- decoded: bfloat16 [64, 128, 2048], P('dp', None, 'segment'), parts along dimension 0
There are 16 independent parts, one for each index of `dp`. A program takes and returns all parts, laid end to end along the dimension named above; an argument that names none is the same for every part. Nothing has to cross between parts.
Inputs may be any that keep to these rules, and one draw needn't show every extreme that they name: `src_lengths`: keys at positions below a sequence's length are its real tokens. `tgt_lengths`: keys at positions below a sequence's length are its real tokens.
All inputs are finite; a program needn't handle non-finite values.
Results may differ from a plain program's by a relative error of at most 0.015.
Values may be sent and summed in bfloat16 or wider, within the bound.
A program may use at most 64 MiB of HBM per device.

v0:
```python
import jax
import jax.numpy as jnp
from jax import lax
from jax.sharding import PartitionSpec as P

HEAD = 64


epsilon = 1e-06
score_scale = 0.125


def partner_2(value, axis, distance):
    mask = 2**distance
    pairs = [(source, source ^ mask) for source in range(lax.axis_size(axis))]
    return lax.ppermute(value, axis, pairs)


def shifted(value, axis, by):
    length = lax.axis_size(axis)
    pairs = [(i, i + by) for i in range(length) if 0 <= i + by < length]
    return lax.ppermute(value, axis, pairs)


def rms_scale(values, gain_vector):
    return (
        values
        * lax.rsqrt(jnp.mean(values * values, axis=-1, keepdims=True) + epsilon)
        * gain_vector
    )


def attention(queries, key_rows, values, allowed):
    head_count = queries.shape[1] // HEAD
    shaped_q = queries.reshape(queries.shape[0], head_count, HEAD)
    shaped_k = key_rows.reshape(key_rows.shape[0], head_count, HEAD)
    shaped_v = values.reshape(values.shape[0], head_count, HEAD)
    scores = (
        jnp.einsum("qhd,khd->hqk", shaped_q, shaped_k, preferred_element_type=jnp.float32)
        * score_scale
    )
    scores = jnp.where(allowed[None], scores, -1000000000.0)
    weights = jax.nn.softmax(scores, axis=-1).astype(jnp.bfloat16)
    mixture = jnp.einsum("hqk,khd->qhd", weights, shaped_v, preferred_element_type=jnp.float32)
    return mixture.reshape(queries.shape[0], -1).astype(jnp.bfloat16)


def pick_row(array, row_slot):
    return lax.dynamic_index_in_dim(array, row_slot, 0, keepdims=False)


def place_row(array, row_slot, update, keep_flag):
    former = pick_row(array, row_slot)
    return lax.dynamic_update_index_in_dim(array, jnp.where(keep_flag, update, former), row_slot, 0)


def on_device(
    src_embed, tgt_embed, src_lengths, tgt_lengths, attn_in, attn_out, norm_gain, final_gain
):
    segments = lax.axis_size("segment")
    group_size = segments // 4
    bit_count = group_size.bit_length() - 1
    segment_index = lax.axis_index("segment")
    section = segment_index // group_size
    member = segment_index % group_size
    batches, seq_len, column_share = src_embed.shape
    full_width = column_share * segments
    destination = (jnp.arange(segments, dtype=jnp.int32) // group_size)[None, None, :, None]
    outgoing = jnp.where(
        destination == 0,
        src_embed[:, :, None, :],
        jnp.where(destination == 2, tgt_embed[:, :, None, :], jnp.zeros((), jnp.bfloat16)),
    )
    arrived = lax.all_to_all(outgoing, "segment", split_axis=2, concat_axis=2, tiled=True)
    embedded = arrived.reshape(batches, seq_len, full_width)
    in_weight = attn_in[0]
    out_weight = attn_out[0]
    head_cols = out_weight.shape[0]
    layer_gain = pick_row(norm_gain, section)
    positions = jnp.arange(seq_len, dtype=jnp.int32)
    causal = positions[None, :] <= positions[:, None]
    is_target = section == 3
    starts_chain = (section == 0) | (section == 2)

    def allowed_for(batch_slot):
        seq_length = jnp.where(
            is_target, pick_row(tgt_lengths, batch_slot), pick_row(src_lengths, batch_slot)
        )
        return (positions[None, :] < seq_length) & (causal | jnp.logical_not(is_target))

    def head_partial(current, memory, batch_slot):
        normed = rms_scale(current.astype(jnp.float32), layer_gain).astype(jnp.bfloat16)
        source = jnp.where(section == 2, memory, normed)
        queries = jnp.dot(
            normed, in_weight[:, :head_cols], preferred_element_type=jnp.float32
        ).astype(jnp.bfloat16)
        key_value = jnp.dot(
            source, in_weight[:, head_cols:], preferred_element_type=jnp.float32
        ).astype(jnp.bfloat16)
        mixture = attention(
            queries, key_value[:, :head_cols], key_value[:, head_cols:], allowed_for(batch_slot)
        )
        return jnp.dot(mixture, out_weight, preferred_element_type=jnp.float32)

    def combine_heads(current, partial_sum):
        retained = partial_sum
        row_start = jnp.zeros((), jnp.int32)
        for bit_index in range(bit_count):
            half_rows = retained.shape[0] // 2
            upper_side = member // (1 << bit_index) % 2 == 1
            sending = jnp.where(upper_side, retained[:half_rows], retained[half_rows:])
            retained = jnp.where(
                upper_side, retained[half_rows:], retained[:half_rows]
            ) + partner_2(sending.astype(jnp.bfloat16), "segment", bit_index).astype(sending.dtype)
            row_start = row_start + jnp.where(upper_side, half_rows, 0).astype(jnp.int32)
        own_rows = lax.dynamic_slice_in_dim(current, row_start, retained.shape[0], 0)
        joined = (own_rows.astype(jnp.float32) + retained).astype(jnp.bfloat16)
        for bit_index in reversed(range(bit_count)):
            upper_side = member // (1 << bit_index) % 2 == 1
            partner = partner_2(joined, "segment", bit_index)
            joined = jnp.concatenate(
                [jnp.where(upper_side, partner, joined), jnp.where(upper_side, joined, partner)],
                axis=0,
            )
        return joined

    def final_norm(output):
        return rms_scale(output.astype(jnp.float32), final_gain).astype(jnp.bfloat16)

    zero_sum = jnp.zeros((seq_len, full_width), jnp.float32)

    def run_sublayer(step_index, received):
        slot_raw = step_index - section
        active = (slot_raw >= 0) & (slot_raw < batches)
        batch_slot = jnp.clip(slot_raw, 0, batches - 1)
        current = jnp.where(starts_chain, pick_row(embedded, batch_slot), received)
        partial_sum = lax.cond(
            active,
            lambda value_in, memory_in: head_partial(value_in, memory_in, batch_slot),
            lambda value_in, memory_in: zero_sum,
            current,
            received,
        )
        output = combine_heads(current, partial_sum)
        return (output, batch_slot, active)

    empty_rows = jnp.zeros((seq_len, full_width), jnp.bfloat16)
    collected = jnp.zeros((batches, seq_len, full_width), jnp.bfloat16)

    def relay_step(step_index, state_tuple):
        received, outputs = state_tuple
        output, batch_slot, active = run_sublayer(step_index, received)
        outputs = place_row(outputs, batch_slot, output, active & (section == 3))
        leaving = jnp.where(section == 1, final_norm(output), output)
        forwarded = shifted(leaving, "segment", group_size)
        return (forwarded, outputs)

    state_tuple = lax.fori_loop(0, batches + 3, relay_step, (empty_rows, collected))
    outputs = state_tuple[1]
    decoded_cols = lax.dynamic_slice_in_dim(outputs, segment_index * column_share, column_share, 2)
    for distance in range(1, 4):
        chosen = lax.dynamic_slice_in_dim(
            outputs, ((3 - distance) * group_size + member) * column_share, column_share, 2
        )
        incoming = shifted(chosen, "segment", -distance * group_size)
        decoded_cols = jnp.where(section == 3 - distance, incoming, decoded_cols)
    return decoded_cols


def solution(mesh):
    in_specs = (
        P("dp", None, "segment"),
        P("dp", None, "segment"),
        P("dp"),
        P("dp"),
        P("segment", None, None),
        P("segment", None, None),
        P(),
        P(),
    )
    out_specs = P("dp", None, "segment")
    return jax.shard_map(
        on_device, mesh=mesh, in_specs=in_specs, out_specs=out_specs, check_vma=False
    )
```

profile of v0, /device:TPU:32, one launch (start us, length us, event | category | flops | bytes accessed | tf_op | source)
XLA Modules:
  0.0 495.4 jit_solution(16149081509362192200)
XLA Ops:
  2.6 9.5 %all-to-all-start = ((bf16[4,128,16,128]{3,1,0,2:T(8,128)(2,1)}), bf16[4,128,16,128]{3,1,0,2:T(8,128)(2,1)S(1)}, u32[]{:S(2)}, u32[]{:S(2)}) async-start(bf16[4,128,16,128]{3,1,0,2:T(8,128)(2,1)} %select_select_fusion), calls=%async_computation | async-start | bytes 4194304 | tf_op jit(solution)/shard_map/all_to_all | solution.py:74
  12.1 48.0 %all-to-all-done = bf16[4,128,16,128]{3,1,0,2:T(8,128)(2,1)S(1)} async-done(((bf16[4,128,16,128]{3,1,0,2:T(8,128)(2,1)}), bf16[4,128,16,128]{3,1,0,2:T(8,128)(2,1)S(1)}, u32[]{:S(2)}, u32[]{:S(2)}) %all-to-all-start) | async-done | bytes 2097184 | tf_op jit(solution)/shard_map/all_to_all | solution.py:74
  64.3 412.1 %while.20 = (s32[]{:T(128)}, bf16[128,2048]{1,0:T(8,128)(2,1)S(1)}, bf16[4,128,2048]{2,1,0:T(8,128)(2,1)}, pred[]{:T(512)}, pred[]{:T(512)}, /*index=5*/pred[]{:...) while((s32[]{:T(128)}, bf16[128,2048]{1,0:T(8,128)(2,1)S(1)}, ...), condition=%wide.region_7.8_spmd.clone, body=%wide.region_0.7_spmd.clone.sunk | while | flops 1136641664 | bytes 44653500 | solution.py:158
  65.8 11.3 %conditional.3 = (f32[64,2048]{1,0:T(8,128)S(1)}, f32[64,2048]{1,0:T(8,128)S(1)}) conditional(s32[]{:T(128)} %convert_element_type.194, () %tuple.74, (s32[]{:T(128)}, bf16[128,2048]{1,0:T(8,128)(2,1)S(1)}, f32[2048]{0:T(1024)S(1)}, bf16[128,2048]{1,0:T(8,128)(2,1)S(1)}, bf16[2048,1536]{1,0:T(8,128)(2,1)}, /*index=5*/s32[]{:T(128)}, s32[4]{0:T(128)S(1)}, ...), branch_computations={%region_1.1_spmd, %region_2.5_spmd} | conditional | flops 1128711680 | bytes 25898372 | solution.py:137
  77.7 6.4 %collective-permute-done = bf16[64,2048]{1,0:T(8,128)(2,1)S(1)} collective-permute-done((bf16[64,2048]{1,0:T(8,128)(2,1)S(1)}, bf16[64,2048]{1,0:T(8,128)(2,1)S(1)}, u32[]{:S(2)}, u32[]{:S(2)}) %collective-permute-start) | collective-permute-done | bytes 262176 | tf_op jit(solution)/shard_map/while/body/eval_jaxpr/ppermute | solution.py:16
  96.1 5.7 %collective-permute-done.3 = bf16[64,2048]{1,0:T(8,128)(2,1)S(1)} collective-permute-done((bf16[64,2048]{1,0:T(8,128)(2,1)S(1)}, bf16[64,2048]{1,0:T(8,128)(2,1)S(1)}, u32[]{:S(2)}, u32[]{:S(2)}) %collective-permute-start.3) | collective-permute-done | bytes 262176 | tf_op jit(solution)/shard_map/while/body/eval_jaxpr/ppermute | solution.py:16
  105.7 15.0 %collective-permute-done.4 = bf16[128,2048]{1,0:T(8,128)(2,1)S(1)} collective-permute-done((bf16[128,2048]{1,0:T(8,128)(2,1)S(1)}, bf16[128,2048]{1,0:T(8,128)(2,1)S(1)}, u32[]{:S(2)}, u32[]{:S(2)}) %collective-permute-start.4) | collective-permute-done | bytes 524320 | tf_op jit(solution)/shard_map/while/body/eval_jaxpr/ppermute | solution.py:22
  122.1 11.3 %conditional.3 = (f32[64,2048]{1,0:T(8,128)S(1)}, f32[64,2048]{1,0:T(8,128)S(1)}) conditional(s32[]{:T(128)} %convert_element_type.194, () %tuple.74, (s32[]{:T(128)}, bf16[128,2048]{1,0:T(8,128)(2,1)S(1)}, f32[2048]{0:T(1024)S(1)}, bf16[128,2048]{1,0:T(8,128)(2,1)S(1)}, bf16[2048,1536]{1,0:T(8,128)(2,1)}, /*index=5*/s32[]{:T(128)}, s32[4]{0:T(128)S(1)}, ...), branch_computations={%region_1.1_spmd, %region_2.5_spmd} | conditional | flops 1128711680 | bytes 25898372 | solution.py:137
  134.1 6.9 %collective-permute-done = bf16[64,2048]{1,0:T(8,128)(2,1)S(1)} collective-permute-done((bf16[64,2048]{1,0:T(8,128)(2,1)S(1)}, bf16[64,2048]{1,0:T(8,128)(2,1)S(1)}, u32[]{:S(2)}, u32[]{:S(2)}) %collective-permute-start) | collective-permute-done | bytes 262176 | tf_op jit(solution)/shard_map/while/body/eval_jaxpr/ppermute | solution.py:16
  152.0 5.8 %collective-permute-done.3 = bf16[64,2048]{1,0:T(8,128)(2,1)S(1)} collective-permute-done((bf16[64,2048]{1,0:T(8,128)(2,1)S(1)}, bf16[64,2048]{1,0:T(8,128)(2,1)S(1)}, u32[]{:S(2)}, u32[]{:S(2)}) %collective-permute-start.3) | collective-permute-done | bytes 262176 | tf_op jit(solution)/shard_map/while/body/eval_jaxpr/ppermute | solution.py:16
  165.7 15.1 %collective-permute-done.4 = bf16[128,2048]{1,0:T(8,128)(2,1)S(1)} collective-permute-done((bf16[128,2048]{1,0:T(8,128)(2,1)S(1)}, bf16[128,2048]{1,0:T(8,128)(2,1)S(1)}, u32[]{:S(2)}, u32[]{:S(2)}) %collective-permute-start.4) | collective-permute-done | bytes 524320 | tf_op jit(solution)/shard_map/while/body/eval_jaxpr/ppermute | solution.py:22
  182.2 11.3 %conditional.3 = (f32[64,2048]{1,0:T(8,128)S(1)}, f32[64,2048]{1,0:T(8,128)S(1)}) conditional(s32[]{:T(128)} %convert_element_type.194, () %tuple.74, (s32[]{:T(128)}, bf16[128,2048]{1,0:T(8,128)(2,1)S(1)}, f32[2048]{0:T(1024)S(1)}, bf16[128,2048]{1,0:T(8,128)(2,1)S(1)}, bf16[2048,1536]{1,0:T(8,128)(2,1)}, /*index=5*/s32[]{:T(128)}, s32[4]{0:T(128)S(1)}, ...), branch_computations={%region_1.1_spmd, %region_2.5_spmd} | conditional | flops 1128711680 | bytes 25898372 | solution.py:137
  194.0 7.8 %collective-permute-done = bf16[64,2048]{1,0:T(8,128)(2,1)S(1)} collective-permute-done((bf16[64,2048]{1,0:T(8,128)(2,1)S(1)}, bf16[64,2048]{1,0:T(8,128)(2,1)S(1)}, u32[]{:S(2)}, u32[]{:S(2)}) %collective-permute-start) | collective-permute-done | bytes 262176 | tf_op jit(solution)/shard_map/while/body/eval_jaxpr/ppermute | solution.py:16
  212.5 6.1 %collective-permute-done.3 = bf16[64,2048]{1,0:T(8,128)(2,1)S(1)} collective-permute-done((bf16[64,2048]{1,0:T(8,128)(2,1)S(1)}, bf16[64,2048]{1,0:T(8,128)(2,1)S(1)}, u32[]{:S(2)}, u32[]{:S(2)}) %collective-permute-start.3) | collective-permute-done | bytes 262176 | tf_op jit(solution)/shard_map/while/body/eval_jaxpr/ppermute | solution.py:16
  226.5 15.9 %collective-permute-done.4 = bf16[128,2048]{1,0:T(8,128)(2,1)S(1)} collective-permute-done((bf16[128,2048]{1,0:T(8,128)(2,1)S(1)}, bf16[128,2048]{1,0:T(8,128)(2,1)S(1)}, u32[]{:S(2)}, u32[]{:S(2)}) %collective-permute-start.4) | collective-permute-done | bytes 524320 | tf_op jit(solution)/shard_map/while/body/eval_jaxpr/ppermute | solution.py:22
  243.7 11.3 %conditional.3 = (f32[64,2048]{1,0:T(8,128)S(1)}, f32[64,2048]{1,0:T(8,128)S(1)}) conditional(s32[]{:T(128)} %convert_element_type.194, () %tuple.74, (s32[]{:T(128)}, bf16[128,2048]{1,0:T(8,128)(2,1)S(1)}, f32[2048]{0:T(1024)S(1)}, bf16[128,2048]{1,0:T(8,128)(2,1)S(1)}, bf16[2048,1536]{1,0:T(8,128)(2,1)}, /*index=5*/s32[]{:T(128)}, s32[4]{0:T(128)S(1)}, ...), branch_computations={%region_1.1_spmd, %region_2.5_spmd} | conditional | flops 1128711680 | bytes 25898372 | solution.py:137
  255.5 8.0 %collective-permute-done = bf16[64,2048]{1,0:T(8,128)(2,1)S(1)} collective-permute-done((bf16[64,2048]{1,0:T(8,128)(2,1)S(1)}, bf16[64,2048]{1,0:T(8,128)(2,1)S(1)}, u32[]{:S(2)}, u32[]{:S(2)}) %collective-permute-start) | collective-permute-done | bytes 262176 | tf_op jit(solution)/shard_map/while/body/eval_jaxpr/ppermute | solution.py:16
  274.2 6.1 %collective-permute-done.3 = bf16[64,2048]{1,0:T(8,128)(2,1)S(1)} collective-permute-done((bf16[64,2048]{1,0:T(8,128)(2,1)S(1)}, bf16[64,2048]{1,0:T(8,128)(2,1)S(1)}, u32[]{:S(2)}, u32[]{:S(2)}) %collective-permute-start.3) | collective-permute-done | bytes 262176 | tf_op jit(solution)/shard_map/while/body/eval_jaxpr/ppermute | solution.py:16
  288.1 16.0 %collective-permute-done.4 = bf16[128,2048]{1,0:T(8,128)(2,1)S(1)} collective-permute-done((bf16[128,2048]{1,0:T(8,128)(2,1)S(1)}, bf16[128,2048]{1,0:T(8,128)(2,1)S(1)}, u32[]{:S(2)}, u32[]{:S(2)}) %collective-permute-start.4) | collective-permute-done | bytes 524320 | tf_op jit(solution)/shard_map/while/body/eval_jaxpr/ppermute | solution.py:22
  306.1 7.9 %collective-permute-done = bf16[64,2048]{1,0:T(8,128)(2,1)S(1)} collective-permute-done((bf16[64,2048]{1,0:T(8,128)(2,1)S(1)}, bf16[64,2048]{1,0:T(8,128)(2,1)S(1)}, u32[]{:S(2)}, u32[]{:S(2)}) %collective-permute-start) | collective-permute-done | bytes 262176 | tf_op jit(solution)/shard_map/while/body/eval_jaxpr/ppermute | solution.py:16
  324.7 6.1 %collective-permute-done.3 = bf16[64,2048]{1,0:T(8,128)(2,1)S(1)} collective-permute-done((bf16[64,2048]{1,0:T(8,128)(2,1)S(1)}, bf16[64,2048]{1,0:T(8,128)(2,1)S(1)}, u32[]{:S(2)}, u32[]{:S(2)}) %collective-permute-start.3) | collective-permute-done | bytes 262176 | tf_op jit(solution)/shard_map/while/body/eval_jaxpr/ppermute | solution.py:16
  331.4 16.5 %collective-permute-start.4 = (bf16[128,2048]{1,0:T(8,128)(2,1)S(1)}, bf16[128,2048]{1,0:T(8,128)(2,1)S(1)}, u32[]{:S(2)}, u32[]{:S(2)}) collective-permute-start(bf16[128,2048]{1,0:T(8,128)(2,1)S(1)} %fusion.50), channel_id=1, source_target_pairs={{0,64},{16,80},{32,96},{48,112},{64,128},{80,144},{96,160},{112,17... | collective-permute-start | bytes 1572872 | tf_op jit(solution)/shard_map/while/body/eval_jaxpr/ppermute | solution.py:22
  349.9 16.0 %collective-permute-done.4 = bf16[128,2048]{1,0:T(8,128)(2,1)S(1)} collective-permute-done((bf16[128,2048]{1,0:T(8,128)(2,1)S(1)}, bf16[128,2048]{1,0:T(8,128)(2,1)S(1)}, u32[]{:S(2)}, u32[]{:S(2)}) %collective-permute-start.4) | collective-permute-done | bytes 524320 | tf_op jit(solution)/shard_map/while/body/eval_jaxpr/ppermute | solution.py:22
  367.9 7.9 %collective-permute-done = bf16[64,2048]{1,0:T(8,128)(2,1)S(1)} collective-permute-done((bf16[64,2048]{1,0:T(8,128)(2,1)S(1)}, bf16[64,2048]{1,0:T(8,128)(2,1)S(1)}, u32[]{:S(2)}, u32[]{:S(2)}) %collective-permute-start) | collective-permute-done | bytes 262176 | tf_op jit(solution)/shard_map/while/body/eval_jaxpr/ppermute | solution.py:16
  386.5 6.1 %collective-permute-done.3 = bf16[64,2048]{1,0:T(8,128)(2,1)S(1)} collective-permute-done((bf16[64,2048]{1,0:T(8,128)(2,1)S(1)}, bf16[64,2048]{1,0:T(8,128)(2,1)S(1)}, u32[]{:S(2)}, u32[]{:S(2)}) %collective-permute-start.3) | collective-permute-done | bytes 262176 | tf_op jit(solution)/shard_map/while/body/eval_jaxpr/ppermute | solution.py:16
  400.4 16.0 %collective-permute-done.4 = bf16[128,2048]{1,0:T(8,128)(2,1)S(1)} collective-permute-done((bf16[128,2048]{1,0:T(8,128)(2,1)S(1)}, bf16[128,2048]{1,0:T(8,128)(2,1)S(1)}, u32[]{:S(2)}, u32[]{:S(2)}) %collective-permute-start.4) | collective-permute-done | bytes 524320 | tf_op jit(solution)/shard_map/while/body/eval_jaxpr/ppermute | solution.py:22
  418.4 7.9 %collective-permute-done = bf16[64,2048]{1,0:T(8,128)(2,1)S(1)} collective-permute-done((bf16[64,2048]{1,0:T(8,128)(2,1)S(1)}, bf16[64,2048]{1,0:T(8,128)(2,1)S(1)}, u32[]{:S(2)}, u32[]{:S(2)}) %collective-permute-start) | collective-permute-done | bytes 262176 | tf_op jit(solution)/shard_map/while/body/eval_jaxpr/ppermute | solution.py:16
  437.1 6.1 %collective-permute-done.3 = bf16[64,2048]{1,0:T(8,128)(2,1)S(1)} collective-permute-done((bf16[64,2048]{1,0:T(8,128)(2,1)S(1)}, bf16[64,2048]{1,0:T(8,128)(2,1)S(1)}, u32[]{:S(2)}, u32[]{:S(2)}) %collective-permute-start.3) | collective-permute-done | bytes 262176 | tf_op jit(solution)/shard_map/while/body/eval_jaxpr/ppermute | solution.py:16
  443.7 15.4 %collective-permute-start.4 = (bf16[128,2048]{1,0:T(8,128)(2,1)S(1)}, bf16[128,2048]{1,0:T(8,128)(2,1)S(1)}, u32[]{:S(2)}, u32[]{:S(2)}) collective-permute-start(bf16[128,2048]{1,0:T(8,128)(2,1)S(1)} %fusion.50), channel_id=1, source_target_pairs={{0,64},{16,80},{32,96},{48,112},{64,128},{80,144},{96,160},{112,17... | collective-permute-start | bytes 1572872 | tf_op jit(solution)/shard_map/while/body/eval_jaxpr/ppermute | solution.py:22
  461.1 15.4 %collective-permute-done.4 = bf16[128,2048]{1,0:T(8,128)(2,1)S(1)} collective-permute-done((bf16[128,2048]{1,0:T(8,128)(2,1)S(1)}, bf16[128,2048]{1,0:T(8,128)(2,1)S(1)}, u32[]{:S(2)}, u32[]{:S(2)}) %collective-permute-start.4) | collective-permute-done | bytes 524320 | tf_op jit(solution)/shard_map/while/body/eval_jaxpr/ppermute | solution.py:22
  481.5 5.5 %collective-permute-done.5 = bf16[4,128,128]{2,1,0:T(8,128)(2,1)S(1)} collective-permute-done((bf16[4,128,128]{2,1,0:T(8,128)(2,1)S(1)}, bf16[4,128,128]{2,1,0:T(8,128)(2,1)S(1)}, u32[]{:S(2)}, u32[]{:S(2)}) %collective-permute-start.5) | collective-permute-done | bytes 131104 | tf_op jit(solution)/shard_map/ppermute | solution.py:22
  487.0 6.8 %collective-permute-done.6 = bf16[4,128,128]{2,1,0:T(8,128)(2,1)S(1)} collective-permute-done((bf16[4,128,128]{2,1,0:T(8,128)(2,1)S(1)}, bf16[4,128,128]{2,1,0:T(8,128)(2,1)S(1)}, u32[]{:S(2)}, u32[]{:S(2)}) %collective-permute-start.6) | collective-permute-done | bytes 131104 | tf_op jit(solution)/shard_map/ppermute | solution.py:22
  (271 shorter events, 183.1 us)
Async XLA Ops:
  2.6 57.5 %all-to-all-start = ((bf16[4,128,16,128]{3,1,0,2:T(8,128)(2,1)}), bf16[4,128,16,128]{3,1,0,2:T(8,128)(2,1)S(1)}, u32[]{:S(2)}, u32[]{:S(2)}) async-start(bf16[4,128,16,128]{3,1,0,2:T(8,128)(2,1)} %select_select_fusion), calls=%async_computation | async-start | bytes 4194304 | tf_op jit(solution)/shard_map/all_to_all | solution.py:74
  77.2 6.9 %collective-permute-start = (bf16[64,2048]{1,0:T(8,128)(2,1)S(1)}, bf16[64,2048]{1,0:T(8,128)(2,1)S(1)}, u32[]{:S(2)}, u32[]{:S(2)}) collective-permute-start(bf16[64,2048]{1,0:T(8,128)(2,1)S(1)} %select_convert_fusion.4), channel_id=1, source_target_pairs={{0,16},{16,0},{32,48},{48,32},{64,80},{80,64},{96,112},{112,96},{1... | collective-permute-start | bytes 786440 | tf_op jit(solution)/shard_map/while/body/eval_jaxpr/ppermute | solution.py:16
  84.2 6.0 %collective-permute-start.1 = (bf16[32,2048]{1,0:T(8,128)(2,1)S(1)}, bf16[32,2048]{1,0:T(8,128)(2,1)S(1)}, u32[]{:S(2)}, u32[]{:S(2)}) collective-permute-start(bf16[32,2048]{1,0:T(8,128)(2,1)S(1)} %select_convert_fusion.5), channel_id=1, source_target_pairs={{0,32},{16,48},{32,0},{48,16},{64,96},{80,112},{96,64},{112,80},{1... | collective-permute-start | bytes 393224 | tf_op jit(solution)/shard_map/while/body/eval_jaxpr/ppermute | solution.py:16
  90.2 5.1 %collective-permute-start.2 = (bf16[32,2048]{1,0:T(8,128)(2,1)S(1)}, bf16[32,2048]{1,0:T(8,128)(2,1)S(1)}, u32[]{:S(2)}, u32[]{:S(2)}) collective-permute-start(bf16[32,2048]{1,0:T(8,128)(2,1)S(1)} %add_convert_fusion.2), channel_id=1, source_target_pairs={{0,32},{16,48},{32,0},{48,16},{64,96},{80,112},{96,64},{112,80},{1... | collective-permute-start | bytes 393224 | tf_op jit(solution)/shard_map/while/body/eval_jaxpr/ppermute | solution.py:16
  95.3 6.5 %collective-permute-start.3 = (bf16[64,2048]{1,0:T(8,128)(2,1)S(1)}, bf16[64,2048]{1,0:T(8,128)(2,1)S(1)}, u32[]{:S(2)}, u32[]{:S(2)}) collective-permute-start(bf16[64,2048]{1,0:T(8,128)(2,1)S(1)} %pad_maximum_fusion.3), channel_id=1, source_target_pairs={{0,16},{16,0},{32,48},{48,32},{64,80},{80,64},{96,112},{112,96},{1... | collective-permute-start | bytes 786440 | tf_op jit(solution)/shard_map/while/body/eval_jaxpr/ppermute | solution.py:16
  102.4 18.3 %collective-permute-start.4 = (bf16[128,2048]{1,0:T(8,128)(2,1)S(1)}, bf16[128,2048]{1,0:T(8,128)(2,1)S(1)}, u32[]{:S(2)}, u32[]{:S(2)}) collective-permute-start(bf16[128,2048]{1,0:T(8,128)(2,1)S(1)} %fusion.50), channel_id=1, source_target_pairs={{0,64},{16,80},{32,96},{48,112},{64,128},{80,144},{96,160},{112,17... | collective-permute-start | bytes 1572872 | tf_op jit(solution)/shard_map/while/body/eval_jaxpr/ppermute | solution.py:22
  133.5 7.5 %collective-permute-start = (bf16[64,2048]{1,0:T(8,128)(2,1)S(1)}, bf16[64,2048]{1,0:T(8,128)(2,1)S(1)}, u32[]{:S(2)}, u32[]{:S(2)}) collective-permute-start(bf16[64,2048]{1,0:T(8,128)(2,1)S(1)} %select_convert_fusion.4), channel_id=1, source_target_pairs={{0,16},{16,0},{32,48},{48,32},{64,80},{80,64},{96,112},{112,96},{1... | collective-permute-start | bytes 786440 | tf_op jit(solution)/shard_map/while/body/eval_jaxpr/ppermute | solution.py:16
  141.1 5.1 %collective-permute-start.1 = (bf16[32,2048]{1,0:T(8,128)(2,1)S(1)}, bf16[32,2048]{1,0:T(8,128)(2,1)S(1)}, u32[]{:S(2)}, u32[]{:S(2)}) collective-permute-start(bf16[32,2048]{1,0:T(8,128)(2,1)S(1)} %select_convert_fusion.5), channel_id=1, source_target_pairs={{0,32},{16,48},{32,0},{48,16},{64,96},{80,112},{96,64},{112,80},{1... | collective-permute-start | bytes 393224 | tf_op jit(solution)/shard_map/while/body/eval_jaxpr/ppermute | solution.py:16
  146.3 5.1 %collective-permute-start.2 = (bf16[32,2048]{1,0:T(8,128)(2,1)S(1)}, bf16[32,2048]{1,0:T(8,128)(2,1)S(1)}, u32[]{:S(2)}, u32[]{:S(2)}) collective-permute-start(bf16[32,2048]{1,0:T(8,128)(2,1)S(1)} %add_convert_fusion.2), channel_id=1, source_target_pairs={{0,32},{16,48},{32,0},{48,16},{64,96},{80,112},{96,64},{112,80},{1... | collective-permute-start | bytes 393224 | tf_op jit(solution)/shard_map/while/body/eval_jaxpr/ppermute | solution.py:16
  151.4 6.5 %collective-permute-start.3 = (bf16[64,2048]{1,0:T(8,128)(2,1)S(1)}, bf16[64,2048]{1,0:T(8,128)(2,1)S(1)}, u32[]{:S(2)}, u32[]{:S(2)}) collective-permute-start(bf16[64,2048]{1,0:T(8,128)(2,1)S(1)} %pad_maximum_fusion.3), channel_id=1, source_target_pairs={{0,16},{16,0},{32,48},{48,32},{64,80},{80,64},{96,112},{112,96},{1... | collective-permute-start | bytes 786440 | tf_op jit(solution)/shard_map/while/body/eval_jaxpr/ppermute | solution.py:16
  158.4 22.4 %collective-permute-start.4 = (bf16[128,2048]{1,0:T(8,128)(2,1)S(1)}, bf16[128,2048]{1,0:T(8,128)(2,1)S(1)}, u32[]{:S(2)}, u32[]{:S(2)}) collective-permute-start(bf16[128,2048]{1,0:T(8,128)(2,1)S(1)} %fusion.50), channel_id=1, source_target_pairs={{0,64},{16,80},{32,96},{48,112},{64,128},{80,144},{96,160},{112,17... | collective-permute-start | bytes 1572872 | tf_op jit(solution)/shard_map/while/body/eval_jaxpr/ppermute | solution.py:22
  193.6 8.2 %collective-permute-start = (bf16[64,2048]{1,0:T(8,128)(2,1)S(1)}, bf16[64,2048]{1,0:T(8,128)(2,1)S(1)}, u32[]{:S(2)}, u32[]{:S(2)}) collective-permute-start(bf16[64,2048]{1,0:T(8,128)(2,1)S(1)} %select_convert_fusion.4), channel_id=1, source_target_pairs={{0,16},{16,0},{32,48},{48,32},{64,80},{80,64},{96,112},{112,96},{1... | collective-permute-start | bytes 786440 | tf_op jit(solution)/shard_map/while/body/eval_jaxpr/ppermute | solution.py:16
  201.9 5.1 %collective-permute-start.1 = (bf16[32,2048]{1,0:T(8,128)(2,1)S(1)}, bf16[32,2048]{1,0:T(8,128)(2,1)S(1)}, u32[]{:S(2)}, u32[]{:S(2)}) collective-permute-start(bf16[32,2048]{1,0:T(8,128)(2,1)S(1)} %select_convert_fusion.5), channel_id=1, source_target_pairs={{0,32},{16,48},{32,0},{48,16},{64,96},{80,112},{96,64},{112,80},{1... | collective-permute-start | bytes 393224 | tf_op jit(solution)/shard_map/while/body/eval_jaxpr/ppermute | solution.py:16
  207.0 5.1 %collective-permute-start.2 = (bf16[32,2048]{1,0:T(8,128)(2,1)S(1)}, bf16[32,2048]{1,0:T(8,128)(2,1)S(1)}, u32[]{:S(2)}, u32[]{:S(2)}) collective-permute-start(bf16[32,2048]{1,0:T(8,128)(2,1)S(1)} %add_convert_fusion.2), channel_id=1, source_target_pairs={{0,32},{16,48},{32,0},{48,16},{64,96},{80,112},{96,64},{112,80},{1... | collective-permute-start | bytes 393224 | tf_op jit(solution)/shard_map/while/body/eval_jaxpr/ppermute | solution.py:16
  212.1 6.5 %collective-permute-start.3 = (bf16[64,2048]{1,0:T(8,128)(2,1)S(1)}, bf16[64,2048]{1,0:T(8,128)(2,1)S(1)}, u32[]{:S(2)}, u32[]{:S(2)}) collective-permute-start(bf16[64,2048]{1,0:T(8,128)(2,1)S(1)} %pad_maximum_fusion.3), channel_id=1, source_target_pairs={{0,16},{16,0},{32,48},{48,32},{64,80},{80,64},{96,112},{112,96},{1... | collective-permute-start | bytes 786440 | tf_op jit(solution)/shard_map/while/body/eval_jaxpr/ppermute | solution.py:16
  219.2 23.2 %collective-permute-start.4 = (bf16[128,2048]{1,0:T(8,128)(2,1)S(1)}, bf16[128,2048]{1,0:T(8,128)(2,1)S(1)}, u32[]{:S(2)}, u32[]{:S(2)}) collective-permute-start(bf16[128,2048]{1,0:T(8,128)(2,1)S(1)} %fusion.50), channel_id=1, source_target_pairs={{0,64},{16,80},{32,96},{48,112},{64,128},{80,144},{96,160},{112,17... | collective-permute-start | bytes 1572872 | tf_op jit(solution)/shard_map/while/body/eval_jaxpr/ppermute | solution.py:22
  255.1 8.3 %collective-permute-start = (bf16[64,2048]{1,0:T(8,128)(2,1)S(1)}, bf16[64,2048]{1,0:T(8,128)(2,1)S(1)}, u32[]{:S(2)}, u32[]{:S(2)}) collective-permute-start(bf16[64,2048]{1,0:T(8,128)(2,1)S(1)} %select_convert_fusion.4), channel_id=1, source_target_pairs={{0,16},{16,0},{32,48},{48,32},{64,80},{80,64},{96,112},{112,96},{1... | collective-permute-start | bytes 786440 | tf_op jit(solution)/shard_map/while/body/eval_jaxpr/ppermute | solution.py:16
  263.6 5.1 %collective-permute-start.1 = (bf16[32,2048]{1,0:T(8,128)(2,1)S(1)}, bf16[32,2048]{1,0:T(8,128)(2,1)S(1)}, u32[]{:S(2)}, u32[]{:S(2)}) collective-permute-start(bf16[32,2048]{1,0:T(8,128)(2,1)S(1)} %select_convert_fusion.5), channel_id=1, source_target_pairs={{0,32},{16,48},{32,0},{48,16},{64,96},{80,112},{96,64},{112,80},{1... | collective-permute-start | bytes 393224 | tf_op jit(solution)/shard_map/while/body/eval_jaxpr/ppermute | solution.py:16
  273.8 6.5 %collective-permute-start.3 = (bf16[64,2048]{1,0:T(8,128)(2,1)S(1)}, bf16[64,2048]{1,0:T(8,128)(2,1)S(1)}, u32[]{:S(2)}, u32[]{:S(2)}) collective-permute-start(bf16[64,2048]{1,0:T(8,128)(2,1)S(1)} %pad_maximum_fusion.3), channel_id=1, source_target_pairs={{0,16},{16,0},{32,48},{48,32},{64,80},{80,64},{96,112},{112,96},{1... | collective-permute-start | bytes 786440 | tf_op jit(solution)/shard_map/while/body/eval_jaxpr/ppermute | solution.py:16
  280.8 23.3 %collective-permute-start.4 = (bf16[128,2048]{1,0:T(8,128)(2,1)S(1)}, bf16[128,2048]{1,0:T(8,128)(2,1)S(1)}, u32[]{:S(2)}, u32[]{:S(2)}) collective-permute-start(bf16[128,2048]{1,0:T(8,128)(2,1)S(1)} %fusion.50), channel_id=1, source_target_pairs={{0,64},{16,80},{32,96},{48,112},{64,128},{80,144},{96,160},{112,17... | collective-permute-start | bytes 1572872 | tf_op jit(solution)/shard_map/while/body/eval_jaxpr/ppermute | solution.py:22
  305.7 8.3 %collective-permute-start = (bf16[64,2048]{1,0:T(8,128)(2,1)S(1)}, bf16[64,2048]{1,0:T(8,128)(2,1)S(1)}, u32[]{:S(2)}, u32[]{:S(2)}) collective-permute-start(bf16[64,2048]{1,0:T(8,128)(2,1)S(1)} %select_convert_fusion.4), channel_id=1, source_target_pairs={{0,16},{16,0},{32,48},{48,32},{64,80},{80,64},{96,112},{112,96},{1... | collective-permute-start | bytes 786440 | tf_op jit(solution)/shard_map/while/body/eval_jaxpr/ppermute | solution.py:16
  324.4 6.5 %collective-permute-start.3 = (bf16[64,2048]{1,0:T(8,128)(2,1)S(1)}, bf16[64,2048]{1,0:T(8,128)(2,1)S(1)}, u32[]{:S(2)}, u32[]{:S(2)}) collective-permute-start(bf16[64,2048]{1,0:T(8,128)(2,1)S(1)} %pad_maximum_fusion.3), channel_id=1, source_target_pairs={{0,16},{16,0},{32,48},{48,32},{64,80},{80,64},{96,112},{112,96},{1... | collective-permute-start | bytes 786440 | tf_op jit(solution)/shard_map/while/body/eval_jaxpr/ppermute | solution.py:16
  331.4 34.5 %collective-permute-start.4 = (bf16[128,2048]{1,0:T(8,128)(2,1)S(1)}, bf16[128,2048]{1,0:T(8,128)(2,1)S(1)}, u32[]{:S(2)}, u32[]{:S(2)}) collective-permute-start(bf16[128,2048]{1,0:T(8,128)(2,1)S(1)} %fusion.50), channel_id=1, source_target_pairs={{0,64},{16,80},{32,96},{48,112},{64,128},{80,144},{96,160},{112,17... | collective-permute-start | bytes 1572872 | tf_op jit(solution)/shard_map/while/body/eval_jaxpr/ppermute | solution.py:22
  367.5 8.3 %collective-permute-start = (bf16[64,2048]{1,0:T(8,128)(2,1)S(1)}, bf16[64,2048]{1,0:T(8,128)(2,1)S(1)}, u32[]{:S(2)}, u32[]{:S(2)}) collective-permute-start(bf16[64,2048]{1,0:T(8,128)(2,1)S(1)} %select_convert_fusion.4), channel_id=1, source_target_pairs={{0,16},{16,0},{32,48},{48,32},{64,80},{80,64},{96,112},{112,96},{1... | collective-permute-start | bytes 786440 | tf_op jit(solution)/shard_map/while/body/eval_jaxpr/ppermute | solution.py:16
  386.1 6.5 %collective-permute-start.3 = (bf16[64,2048]{1,0:T(8,128)(2,1)S(1)}, bf16[64,2048]{1,0:T(8,128)(2,1)S(1)}, u32[]{:S(2)}, u32[]{:S(2)}) collective-permute-start(bf16[64,2048]{1,0:T(8,128)(2,1)S(1)} %pad_maximum_fusion.3), channel_id=1, source_target_pairs={{0,16},{16,0},{32,48},{48,32},{64,80},{80,64},{96,112},{112,96},{1... | collective-permute-start | bytes 786440 | tf_op jit(solution)/shard_map/while/body/eval_jaxpr/ppermute | solution.py:16
  393.2 23.3 %collective-permute-start.4 = (bf16[128,2048]{1,0:T(8,128)(2,1)S(1)}, bf16[128,2048]{1,0:T(8,128)(2,1)S(1)}, u32[]{:S(2)}, u32[]{:S(2)}) collective-permute-start(bf16[128,2048]{1,0:T(8,128)(2,1)S(1)} %fusion.50), channel_id=1, source_target_pairs={{0,64},{16,80},{32,96},{48,112},{64,128},{80,144},{96,160},{112,17... | collective-permute-start | bytes 1572872 | tf_op jit(solution)/shard_map/while/body/eval_jaxpr/ppermute | solution.py:22
  418.0 8.3 %collective-permute-start = (bf16[64,2048]{1,0:T(8,128)(2,1)S(1)}, bf16[64,2048]{1,0:T(8,128)(2,1)S(1)}, u32[]{:S(2)}, u32[]{:S(2)}) collective-permute-start(bf16[64,2048]{1,0:T(8,128)(2,1)S(1)} %select_convert_fusion.4), channel_id=1, source_target_pairs={{0,16},{16,0},{32,48},{48,32},{64,80},{80,64},{96,112},{112,96},{1... | collective-permute-start | bytes 786440 | tf_op jit(solution)/shard_map/while/body/eval_jaxpr/ppermute | solution.py:16
  436.7 6.5 %collective-permute-start.3 = (bf16[64,2048]{1,0:T(8,128)(2,1)S(1)}, bf16[64,2048]{1,0:T(8,128)(2,1)S(1)}, u32[]{:S(2)}, u32[]{:S(2)}) collective-permute-start(bf16[64,2048]{1,0:T(8,128)(2,1)S(1)} %pad_maximum_fusion.3), channel_id=1, source_target_pairs={{0,16},{16,0},{32,48},{48,32},{64,80},{80,64},{96,112},{112,96},{1... | collective-permute-start | bytes 786440 | tf_op jit(solution)/shard_map/while/body/eval_jaxpr/ppermute | solution.py:16
  443.7 32.8 %collective-permute-start.4 = (bf16[128,2048]{1,0:T(8,128)(2,1)S(1)}, bf16[128,2048]{1,0:T(8,128)(2,1)S(1)}, u32[]{:S(2)}, u32[]{:S(2)}) collective-permute-start(bf16[128,2048]{1,0:T(8,128)(2,1)S(1)} %fusion.50), channel_id=1, source_target_pairs={{0,64},{16,80},{32,96},{48,112},{64,128},{80,144},{96,160},{112,17... | collective-permute-start | bytes 1572872 | tf_op jit(solution)/shard_map/while/body/eval_jaxpr/ppermute | solution.py:22
  477.6 9.5 %collective-permute-start.5 = (bf16[4,128,128]{2,1,0:T(8,128)(2,1)S(1)}, bf16[4,128,128]{2,1,0:T(8,128)(2,1)S(1)}, u32[]{:S(2)}, u32[]{:S(2)}) collective-permute-start(bf16[4,128,128]{2,1,0:T(8,128)(2,1)S(1)} %get-tuple-element.859), channel_id=1, source_target_pairs={{192,0},{208,16},{224,32},{240,48},{193,1},{209,17},{225,33},{241,... | collective-permute-start | bytes 393224 | tf_op jit(solution)/shard_map/ppermute | solution.py:22
  478.9 14.9 %collective-permute-start.6 = (bf16[4,128,128]{2,1,0:T(8,128)(2,1)S(1)}, bf16[4,128,128]{2,1,0:T(8,128)(2,1)S(1)}, u32[]{:S(2)}, u32[]{:S(2)}) collective-permute-start(bf16[4,128,128]{2,1,0:T(8,128)(2,1)S(1)} %get-tuple-element.858), channel_id=1, source_target_pairs={{128,0},{144,16},{160,32},{176,48},{192,64},{208,80},{224,96},{240... | collective-permute-start | bytes 393224 | tf_op jit(solution)/shard_map/ppermute | solution.py:22
  480.2 13.6 %collective-permute-start.7 = (bf16[4,128,128]{2,1,0:T(8,128)(2,1)S(1)}, bf16[4,128,128]{2,1,0:T(8,128)(2,1)S(1)}, u32[]{:S(2)}, u32[]{:S(2)}) collective-permute-start(bf16[4,128,128]{2,1,0:T(8,128)(2,1)S(1)} %get-tuple-element.857), channel_id=1, source_target_pairs={{64,0},{80,16},{96,32},{112,48},{128,64},{144,80},{160,96},{176,11... | collective-permute-start | bytes 393224 | tf_op jit(solution)/shard_map/ppermute | solution.py:22
  (15 other events, 60.3 us)
where the time goes:
time: 501 us; the launch traced here: 495 us
  waiting for transfers between devices  331 us (66%)
  starting transfers between devices  79.7 us (16%)
  local copies, waits for them, and re-layouts  27.5 us (5%)
  matrix products  25.7 us (5%)
  other arithmetic  25.1 us (5%)
  loops' own time  6.7 us (1%)
    ppermute x28, waiting for transfers between devices, partner_2(): return lax.ppermute(value, axis, pairs)  161 us
    ppermute x10, waiting for transfers between devices, shifted(): return lax.ppermute(value, axis, pairs)  122 us
    ppermute x10, starting transfers between devices, shifted(): return lax.ppermute(value, axis, pairs)  58.4 us
    all_to_all x1, waiting for transfers between devices, on_device(): lax.all_to_all(outgoing, 'segment', split_axis=2, concat_axis=2, tiled=True)  48 us
    dynamic_slice x23, local copies, waits for them, and re-layouts, pick_row(): return lax.dynamic_index_in_dim(array, row_slot, 0, keepdims=False)  13.8 us
    dynamic_update_slice x7, other arithmetic, place_row(): lax.dynamic_update_index_in_dim(array, jnp.where(keep_flag, update, forme...  13.8 us
    dot_general x4, matrix products, head_partial(): jnp.dot(source, in_weight[:, head_cols:], preferred_element_type=jnp.floa...  11.8 us
    ppermute x28, starting transfers between devices, partner_2(): return lax.ppermute(value, axis, pairs)  11.8 us
  transfers between devices with their start and end apart: 39, of which 38 were waited for; matrix products, arithmetic and copies ran while one was open for 3% of the time, Pallas kernels for 0%

commit v1 on v0

v1 whole, which is shorter than its diff:
```python
import functools

import jax
import jax.numpy as jnp
from jax import lax
from jax.experimental import pallas as pl
from jax.experimental.pallas import tpu as pltpu
from jax.sharding import PartitionSpec as P

HEAD = 64
GROUP = 4
EPS = 1e-06
SCALE = 0.125
MASKED = -1000000000.0
MESH = pl.DeviceIdType.MESH
F32 = jnp.float32
BF16 = jnp.bfloat16


def rms(values, gain):
    return values * lax.rsqrt(jnp.mean(values * values, axis=-1, keepdims=True) + EPS) * gain


def kernel(
    n_seg, src, tgt, slen, tlen, win, wout, gain, fgain, out,
    w_in, w_out, arr, tg, nb, sb, qkv, mix, pf, part, rx, rz, zs, yb,
    wsem, src_send, tgt_send, arr_recv, tgt_recv,
    relay_s, relay_r, agz_s, agz_r, agx_s, agx_r, rsx_s, rsx_r, rsz_s, rsz_r, out_s, out_r,
):
    batches, seq, cols = src.shape
    rows = seq // GROUP
    heads = w_out.shape[0]
    s = lax.axis_index("segment")
    sect = s // GROUP
    m = s % GROUP
    zl = m // 2
    xl = m % 2
    x_near = s + 1 - 2 * xl
    z_near = s + 2 - 4 * zl
    last = n_seg // GROUP - 1

    load_in = pltpu.make_async_copy(win.at[0], w_in, wsem.at[0])
    load_out = pltpu.make_async_copy(wout.at[0], w_out, wsem.at[1])
    load_in.start()
    load_out.start()

    barrier = pltpu.get_barrier_semaphore()
    for k in range(1, n_seg):
        pl.semaphore_signal(
            barrier, inc=1, device_id={"segment": (s + k) % n_seg}, device_id_type=MESH
        )
    pl.semaphore_wait(barrier, n_seg - 1)

    def remote(src_ref, dst_ref, send, recv, target):
        return pltpu.make_async_remote_copy(
            src_ref=src_ref, dst_ref=dst_ref, send_sem=send, recv_sem=recv,
            device_id={"segment": target}, device_id_type=MESH,
        )

    def wait_for(ref, sem):
        pltpu.make_async_copy(ref, ref, sem).wait()

    def quarter(q):
        return pl.ds(pl.multiple_of(q * rows, rows), rows)

    own_cols = pl.ds(pl.multiple_of(s * cols, cols), cols)

    def scatter(given, held, send, recv, first):
        def one(b, carry):
            for t in range(GROUP):
                @pl.when(s != first + t)
                def _():
                    remote(
                        given.at[b], held.at[b, :, own_cols], send.at[b, t], recv.at[b], first + t
                    ).start()

                @pl.when(s == first + t)
                def _():
                    pltpu.make_async_copy(given.at[b], held.at[b, :, own_cols], recv.at[b]).start()
            return carry

        lax.fori_loop(0, batches, one, 0)

    scatter(src, arr, src_send, arr_recv, 0)
    scatter(tgt, tg, tgt_send, tgt_recv, 2 * GROUP)

    def relay(b):
        return remote(
            yb.at[b], arr.at[b, quarter(m)], relay_s.at[b], relay_r.at[b], (s + GROUP) % n_seg
        )

    def gather_z(b):
        part_ref = arr.at[b, quarter(m)]
        return remote(part_ref, part_ref, agz_s.at[b], agz_r.at[b], z_near)

    def gather_x(b, which):
        part_ref = arr.at[b, quarter(m if which == 0 else z_near % GROUP)]
        return remote(part_ref, part_ref, agx_s.at[b, which], agx_r.at[b, which], x_near)

    def sum_x(b, which):
        wanted = x_near % GROUP
        if which == 0:
            wanted = (wanted + 2) % GROUP
        return remote(
            part.at[b, quarter(wanted)], rx.at[b, which], rsx_s.at[b, which], rsx_r.at[b, which], x_near
        )

    def sum_z(b):
        return remote(zs.at[b], rz.at[b], rsz_s.at[b], rsz_r.at[b], z_near)

    def out_copy(b, t):
        return remote(
            yb.at[b, :, pl.ds(pl.multiple_of(t * cols, cols), cols)],
            out.at[b, quarter(m)], out_s.at[b, t], out_r.at[b], t,
        )

    def step_r(b):
        wait_for(arr.at[b, quarter(m)], relay_r.at[b])
        gather_z(b).start()
        gather_x(b, 0).start()

    def step_f(b):
        gather_z(b).wait_recv()
        gather_x(b, 1).start()

    def step_c(b):
        @pl.when(sect == 0)
        def _():
            wait_for(arr.at[b], arr_recv.at[b])

        @pl.when(sect > 0)
        def _():
            gather_x(b, 0).wait_recv()
            gather_x(b, 1).wait_recv()

        own_gain = gain[pl.ds(sect, 1), :]

        @pl.when(sect == 2)
        def _():
            wait_for(tg.at[b], tgt_recv.at[b])
            nb[...] = rms(tg[b].astype(F32), own_gain).astype(BF16)
            sb[...] = arr[b]

        @pl.when(sect != 2)
        def _():
            normed = rms(arr[b].astype(F32), own_gain).astype(BF16)
            nb[...] = normed
            sb[...] = normed

        qkv[:, :heads] = jnp.dot(
            nb[...], w_in[:, :heads], preferred_element_type=F32
        ).astype(BF16)
        qkv[:, heads:] = jnp.dot(
            sb[...], w_in[:, heads:], preferred_element_type=F32
        ).astype(BF16)

        length = jnp.where(sect == last, tlen[b], slen[b])
        query_pos = lax.broadcasted_iota(jnp.int32, (seq, seq), 0)
        key_pos = lax.broadcasted_iota(jnp.int32, (seq, seq), 1)
        limit = jnp.where(sect == last, query_pos, seq)
        allowed = (key_pos < length) & (key_pos <= limit)
        allowed = jnp.concatenate([allowed, allowed], axis=0)
        pair = 2 * HEAD
        low = lax.broadcasted_iota(jnp.int32, (seq, pair), 1) < HEAD
        for j in range(heads // pair):
            q2 = qkv[:, j * pair:(j + 1) * pair]
            k2 = qkv[:, heads + j * pair:heads + (j + 1) * pair]
            v2 = qkv[:, 2 * heads + j * pair:2 * heads + (j + 1) * pair]
            zero = jnp.zeros_like(q2)
            stacked = jnp.concatenate([jnp.where(low, q2, zero), jnp.where(low, zero, q2)], axis=0)
            scores = lax.dot_general(
                stacked, k2, (((1,), (1,)), ((), ())), preferred_element_type=F32
            ) * SCALE
            scores = jnp.where(allowed, scores, MASKED)
            grown = jnp.exp(scores - jnp.max(scores, axis=-1, keepdims=True))
            weights = (grown / jnp.sum(grown, axis=-1, keepdims=True)).astype(BF16)
            both = jnp.dot(weights, v2, preferred_element_type=F32)
            mix[:, j * pair:(j + 1) * pair] = jnp.where(low, both[:seq], both[seq:]).astype(BF16)

        total = jnp.dot(mix[...], w_out[...], preferred_element_type=F32)
        pf[...] = total
        part[b] = total.astype(BF16)
        sum_x(b, 0).start()
        sum_x(b, 1).start()

    def step_z(b):
        sum_x(b, 0).wait_recv()
        zs[b] = (pf[quarter(z_near % GROUP), :] + rx[b, 0].astype(F32)).astype(BF16)
        sum_z(b).start()

    def step_y(b):
        sum_x(b, 1).wait_recv()
        sum_z(b).wait_recv()
        total = pf[quarter(m), :] + rx[b, 1].astype(F32) + rz[b].astype(F32)

        @pl.when(sect == 2)
        def _():
            yb[b] = (tg[b, quarter(m), :].astype(F32) + total).astype(BF16)

        @pl.when(sect == 1)
        def _():
            encoded = (arr[b, quarter(m), :].astype(F32) + total).astype(BF16)
            yb[b] = rms(encoded.astype(F32), fgain[...]).astype(BF16)

        @pl.when((sect != 1) & (sect != 2))
        def _():
            yb[b] = (arr[b, quarter(m), :].astype(F32) + total).astype(BF16)

        @pl.when(sect < last)
        def _():
            relay(b).start()

        @pl.when(sect == last)
        def _():
            def one(t, carry):
                @pl.when(t != s)
                def _():
                    out_copy(b, t).start()

                @pl.when(t == s)
                def _():
                    pltpu.make_async_copy(yb.at[b, :, own_cols], out.at[b, quarter(m)], out_r.at[b]).start()
                return carry

            lax.fori_loop(0, n_seg, one, 0)

    load_in.wait()
    load_out.wait()

    @pl.when(sect > 0)
    def _():
        step_r(0)
        step_f(0)

    def main(b, carry):
        step_c(b)

        @pl.when((sect > 0) & (b < batches - 1))
        def _():
            step_r(b + 1)

        step_z(b)

        @pl.when((sect > 0) & (b < batches - 1))
        def _():
            step_f(b + 1)

        step_y(b)
        return carry

    lax.fori_loop(0, batches, main, 0)

    def finish(b, carry):
        for t in range(GROUP):
            @pl.when(s != t)
            def _():
                remote(src.at[b], arr.at[b, :, own_cols], src_send.at[b, t], arr_recv.at[b], t).wait_send()

            @pl.when(s != 2 * GROUP + t)
            def _():
                remote(
                    tgt.at[b], tg.at[b, :, own_cols], tgt_send.at[b, t], tgt_recv.at[b], 2 * GROUP + t
                ).wait_send()

        sum_x(b, 0).wait_send()
        sum_x(b, 1).wait_send()
        sum_z(b).wait_send()

        @pl.when(sect > 0)
        def _():
            gather_z(b).wait_send()
            gather_x(b, 0).wait_send()
            gather_x(b, 1).wait_send()

        @pl.when(sect < last)
        def _():
            relay(b).wait_send()

        @pl.when(sect == last)
        def _():
            def one(t, inner):
                @pl.when(t != s)
                def _():
                    out_copy(b, t).wait_send()
                return inner

            lax.fori_loop(0, n_seg, one, 0)

        wait_for(out.at[b], out_r.at[b])
        return carry

    lax.fori_loop(0, batches, finish, 0)


def on_device(n_seg, src, tgt, slen, tlen, win, wout, gain, fgain):
    batches, seq, cols = src.shape
    width = cols * n_seg
    depth, fan = win.shape[1:]
    heads = wout.shape[1]
    rows = seq // GROUP
    any_space = pl.BlockSpec(memory_space=pl.ANY)
    vmem = pl.BlockSpec(memory_space=pltpu.VMEM)
    smem = pl.BlockSpec(memory_space=pltpu.SMEM)
    dma = pltpu.SemaphoreType.DMA
    return pl.pallas_call(
        functools.partial(kernel, n_seg),
        out_shape=jax.ShapeDtypeStruct((batches, seq, cols), BF16),
        in_specs=[any_space, any_space, smem, smem, any_space, any_space, vmem, vmem],
        out_specs=any_space,
        scratch_shapes=[
            pltpu.VMEM((depth, fan), BF16),
            pltpu.VMEM((heads, width), BF16),
            pltpu.VMEM((batches, seq, width), BF16),
            pltpu.VMEM((batches, seq, width), BF16),
            pltpu.VMEM((seq, width), BF16),
            pltpu.VMEM((seq, width), BF16),
            pltpu.VMEM((seq, fan), BF16),
            pltpu.VMEM((seq, heads), BF16),
            pltpu.VMEM((seq, width), F32),
            pltpu.VMEM((batches, seq, width), BF16),
            pltpu.VMEM((batches, 2, rows, width), BF16),
            pltpu.VMEM((batches, rows, width), BF16),
            pltpu.VMEM((batches, rows, width), BF16),
            pltpu.VMEM((batches, rows, width), BF16),
            dma((2,)),
            dma((batches, GROUP)), dma((batches, GROUP)), dma((batches,)), dma((batches,)),
            dma((batches,)), dma((batches,)), dma((batches,)), dma((batches,)),
            dma((batches, 2)), dma((batches, 2)), dma((batches, 2)), dma((batches, 2)),
            dma((batches,)), dma((batches,)), dma((batches, n_seg)), dma((batches,)),
        ],
        compiler_params=pltpu.CompilerParams(
            collective_id=0, has_side_effects=True, vmem_limit_bytes=56 * 1024 * 1024
        ),
    )(src, tgt, slen, tlen, win, wout, gain, fgain.reshape(1, -1))


def solution(mesh):
    spec = P("dp", None, "segment")
    return jax.shard_map(
        functools.partial(on_device, mesh.shape["segment"]),
        mesh=mesh,
        in_specs=(spec, spec, P("dp"), P("dp"), P("segment", None, None), P("segment", None, None), P(), P()),
        out_specs=spec,
        check_vma=False,
    )
```

time: 501 us -> 182 us (0.36)
  waiting for transfers between devices: 331 us -> 0 us
  Pallas kernels: 0 us -> 178 us
  starting transfers between devices: 79.7 us -> 0 us
  local copies, waits for them, and re-layouts: 27.5 us -> 1.57 us
  matrix products: 25.7 us -> 0 us
  other arithmetic: 25.1 us -> 0 us
  loops' own time: 6.7 us -> 0 us
    ppermute x38 -> x0, waiting for transfers between devices: 283 us -> none  [the longest x28 161 us: partner_2(): return lax.ppermute(value, axis, pairs)]
    pallas_call x0 -> x1, Pallas kernels: none -> 178 us  [on_device(): pl.pallas_call(functools.partial(kernel, n_seg), out_shape=jax.ShapeDtype...]
    ppermute x38 -> x0, starting transfers between devices: 70.1 us -> none  [the longest x10 58.4 us: shifted(): return lax.ppermute(value, axis, pairs)]
    all_to_all x1 -> x0, waiting for transfers between devices: 48 us -> none  [on_device(): lax.all_to_all(outgoing, 'segment', split_axis=2, concat_axis=2, tiled=True)]
    dot_general x20 -> x0, matrix products: 24.2 us -> none  [the longest x4 11.8 us: head_partial(): jnp.dot(source, in_weight[:, head_cols:], preferred_element_type=jnp.floa...]
    dynamic_slice x24 -> x0, local copies, waits for them, and re-layouts: 14.9 us -> none  [the longest x23 13.8 us: pick_row(): return lax.dynamic_index_in_dim(array, row_slot, 0, keepdims=False)]
    dynamic_update_slice x7 -> x0, other arithmetic: 13.8 us -> none  [place_row(): lax.dynamic_update_index_in_dim(array, jnp.where(keep_flag, update, forme...]
    all_to_all x1 -> x0, starting transfers between devices: 9.51 us -> none  [on_device(): lax.all_to_all(outgoing, 'segment', split_axis=2, concat_axis=2, tiled=True)]
  transfers between devices with their start and end apart: 39 -> 0, of which waited for: 38 -> 0; matrix products, arithmetic and copies ran while one was open for 3% -> 0% of each run, Pallas kernels for 0% -> 0%
where the time goes in v1:
time: 182 us; the launch traced here: 180 us
  Pallas kernels  178 us (98%)
    pallas_call x1, Pallas kernels, on_device(): pl.pallas_call(functools.partial(kernel, n_seg), out_shape=jax.ShapeDtype...  178 us

profile of v1, /device:TPU:32, one launch (start us, length us, event | category | flops | bytes accessed | tf_op | source)
XLA Modules:
  0.0 179.8 jit_solution(11653845437652747640)
XLA Ops:
  0.0 178.2 %shard_map.82 = bf16[4,128,128]{2,1,0:T(8,128)(2,1)} custom-call(bf16[4,128,128]{2,1,0:T(8,128)(2,1)} %src.1, bf16[4,128,128]{2,1,0:T(8,128)(2,1)} %tgt.1, s32[4]{0:T(128)} %slen.1, s32[4]{0:T(128)} %tlen.1, bf16[1,2048,1536]{2,1,0:T(8,128)(2,1)} %win.1, bf16[1,512,2048]{2,1,0:T(8,128)(2,1)} %wout.1, f32[4,2048]{1,0:T(4,128)} %gain.1, f32[1,2048]{1,0:T(1,128)} %bitcast.1), custom_call_target="tpu_custom_call" | custom-call | tf_op jit(solution)/shard_map/pallas_call | solution.py:305
  178.2 1.6 copy.10
